TPU v7x, 32 devices: a whole 2x2x4 slice. The times are simulated.
32 devices in a mesh: groups: 2 (over x), ctx: 16 (over z, y, core).
Axes of the slice: x: 2, y: 2, z: 4, core: 2. Of those that a mesh axis runs over, the one named last changes fastest.
Arguments:
- queries: bfloat16 [96, 4096], P(('groups', 'ctx')), parts along dimension 0, may hold values from -200 to 200
- cache_keys: bfloat16 [4096, 512], P(('groups', 'ctx')), parts along dimension 0, may hold values from -6 to 6
- cache_values: bfloat16 [4096, 512], P(('groups', 'ctx')), parts along dimension 0, may hold values from -6 to 6
- new_keys: bfloat16 [96, 512], P(('groups', 'ctx')), parts along dimension 0, may hold values from -6 to 6
- new_values: bfloat16 [96, 512], P(('groups', 'ctx')), parts along dimension 0, may hold values from -6 to 6
- cache_lengths: int32 [32], P(('groups', 'ctx')), parts along dimension 0, may hold values from 0 to 128, as said below
- residual_in: bfloat16 [96, 2048], P(('groups', 'ctx')), parts along dimension 0, may hold values from -6 to 6
- out_weight: bfloat16 [4096, 2048], P('ctx'), may hold values from -3 to 3
- norm_gain: bfloat16 [2048], replicated, may hold values from 0.25 to 1.75
- expert_gate: bfloat16 [16, 2048, 768], P('ctx'), may hold values from -0.125 to 0.125
- expert_up: bfloat16 [16, 2048, 768], P('ctx'), may hold values from -0.125 to 0.125
- expert_down: bfloat16 [16, 768, 2048], P('ctx'), may hold values from -0.21875 to 0.21875
- expert_ids: int32 [96, 8], P(('groups', 'ctx')), parts along dimension 0, may hold values from 0 to 15, all different within a row; in each aligned block of 3 rows (0 to 2, 3 to 5, ...) at most 3 rows name the same one
- expert_weights: float32 [96, 8], P(('groups', 'ctx')), parts along dimension 0, may hold values from 0.03 to 0.4
Outputs:
- layer_out: bfloat16 [96, 2048], P(('groups', 'ctx')), parts along dimension 0
There are 2 independent parts, one for each index of `groups`. A program takes and returns all parts, laid end to end along the dimension named above; an argument that names none is the same for every part. Nothing has to cross between parts.
Inputs may be any that keep to these rules, and one draw needn't show every extreme that they name: `cache_lengths`: some shard in every draw is full, with 128 live positions. `expert_ids`: within one block of 3 rows no expert is named more than 3 times, a bound that some block reaches.
All inputs are finite; a program needn't handle non-finite values.
Results may differ from a plain program's by a relative error of at most 0.01.
Values may be sent and summed in bfloat16 or wider, within the bound.
No kernel may reach another device: no remote copies, remote signals or barrier semaphores. Data moves between devices by JAX's collectives and lax.ppermute only.
A program may use at most 64 MiB of HBM per device.

v0:
```python
import jax
import jax.numpy as jnp
from jax import lax
from jax.sharding import PartitionSpec as P

HEADS = 32
KV_HEADS = 4
HEAD_DIM = 128
TOP = 8
MASKED = -1e30
epsilon = 1e-06


def local(
    queries,
    cache_keys,
    cache_values,
    new_keys,
    new_values,
    cache_lengths,
    residual_in,
    out_weight,
    norm_gain,
    expert_gate,
    expert_up,
    expert_down,
    expert_ids,
    expert_weights,
):
    shards = lax.axis_size("ctx")
    device = lax.axis_index("ctx")
    rows_dev = residual_in.shape[0]
    capacity = max(2, 2 * rows_dev * TOP // shards)
    group_size = HEADS // KV_HEADS
    whole_queries = lax.all_gather(queries, "ctx", axis=0, tiled=True)
    all_rows = whole_queries.shape[0]
    query_heads = whole_queries.reshape(all_rows, KV_HEADS, group_size, HEAD_DIM)
    local_cache = cache_keys.shape[0]
    key_rows = jnp.concatenate([cache_keys, new_keys], 0).reshape(
        local_cache + rows_dev, KV_HEADS, HEAD_DIM
    )
    value_rows = jnp.concatenate([cache_values, new_values], 0).reshape(
        local_cache + rows_dev, KV_HEADS, HEAD_DIM
    )
    slot_ids = jnp.arange(local_cache + rows_dev, dtype=jnp.int32)
    span_pos = device * rows_dev + slot_ids - local_cache
    row_ids = jnp.arange(all_rows, dtype=jnp.int32)
    usable = jnp.where(
        slot_ids[None, :] < local_cache,
        (slot_ids < cache_lengths[0])[None, :],
        span_pos[None, :] <= row_ids[:, None],
    )
    scores = jnp.einsum(
        "rkgd,nkd->kgrn", query_heads, key_rows, preferred_element_type=jnp.float32
    ) * HEAD_DIM ** (-0.5)
    scores = jnp.where(usable, scores, MASKED)
    maxima = jnp.max(scores, axis=-1)
    exp_weights = jnp.where(usable, jnp.exp(scores - maxima[..., None]), 0.0)
    totals = jnp.sum(exp_weights, axis=-1)
    numerators = jnp.einsum(
        "kgrn,nkd->rkgd",
        exp_weights.astype(jnp.bfloat16),
        value_rows,
        preferred_element_type=jnp.float32,
    ).reshape(all_rows, HEADS, HEAD_DIM)
    maxima = maxima.transpose(2, 0, 1).reshape(all_rows, HEADS)
    totals = totals.transpose(2, 0, 1).reshape(all_rows, HEADS)
    largest = lax.pmax(maxima, "ctx")
    rescale = jnp.exp(maxima - largest)
    denoms = lax.psum(totals * rescale, "ctx")
    weighted = (numerators * (rescale / denoms)[..., None]).reshape(all_rows, HEADS * HEAD_DIM)
    columns = lax.psum_scatter(weighted, "ctx", scatter_dimension=1, tiled=True).astype(
        jnp.bfloat16
    )
    projected = lax.psum_scatter(
        jnp.dot(columns, out_weight, preferred_element_type=jnp.float32),
        "ctx",
        scatter_dimension=0,
        tiled=True,
    )
    state = residual_in.astype(jnp.float32) + projected
    normed = (
        state
        * lax.rsqrt(jnp.mean(state * state, axis=1, keepdims=True) + epsilon)
        * norm_gain.astype(jnp.float32)
    ).astype(jnp.bfloat16)
    n_slots = shards * capacity
    flat_ids = expert_ids.reshape(-1)
    places = jnp.arange(flat_ids.shape[0], dtype=jnp.int32)
    earlier = (flat_ids[:, None] == flat_ids[None, :]) & (places[None, :] < places[:, None])
    slot_of = flat_ids * capacity + jnp.sum(earlier.astype(jnp.int32), axis=1)
    one_hot = (slot_of[:, None] == jnp.arange(n_slots, dtype=jnp.int32)[None, :]).astype(
        jnp.float32
    )
    dispatch_map = one_hot.reshape(rows_dev, TOP, n_slots).sum(1)
    outgoing = (
        jnp.dot(dispatch_map.T.astype(jnp.bfloat16), normed, preferred_element_type=jnp.float32)
        .astype(jnp.bfloat16)
        .reshape(shards, capacity, normed.shape[1])
    )
    received = lax.all_to_all(outgoing, "ctx", split_axis=0, concat_axis=0, tiled=True)
    gate_out = jnp.einsum(
        "scd,df->scf", received, expert_gate[0], preferred_element_type=jnp.float32
    )
    up_out = jnp.einsum("scd,df->scf", received, expert_up[0], preferred_element_type=jnp.float32)
    activated = (jax.nn.silu(gate_out) * up_out).astype(jnp.bfloat16)
    expert_out = jnp.einsum(
        "scf,fd->scd", activated, expert_down[0], preferred_element_type=jnp.float32
    ).astype(jnp.bfloat16)
    back = lax.all_to_all(expert_out, "ctx", split_axis=0, concat_axis=0, tiled=True)
    combine_map = (
        (one_hot * expert_weights.reshape(-1)[:, None]).reshape(rows_dev, TOP, n_slots).sum(1)
    )
    expert_sum = jnp.dot(
        combine_map,
        back.reshape(n_slots, normed.shape[1]).astype(jnp.float32),
        precision=lax.Precision.HIGHEST,
    )
    return (state + expert_sum).astype(jnp.bfloat16)


def solution(mesh):
    placed = (
        P(("groups", "ctx"), None),
        P(("groups", "ctx"), None),
        P(("groups", "ctx"), None),
        P(("groups", "ctx"), None),
        P(("groups", "ctx"), None),
        P(("groups", "ctx")),
        P(("groups", "ctx"), None),
        P("ctx", None),
        P(),
        P("ctx", None, None),
        P("ctx", None, None),
        P("ctx", None, None),
        P(("groups", "ctx"), None),
        P(("groups", "ctx"), None),
    )
    return jax.shard_map(
        local, mesh=mesh, in_specs=placed, out_specs=P(("groups", "ctx"), None), check_vma=False
    )
```

profile of v0, /device:TPU:0, one launch (start us, length us, event | category | flops | bytes accessed | tf_op | source)
XLA Modules:
  0.0 359.6 jit_solution(11415697979822261193)
XLA Ops:
  6.5 0.0 copy-start
  6.5 0.0 reduce-scatter.2.cloned.1.call-start
  7.3 0.6 add_add_fusion
  7.9 0.6 iota_compare_fusion.3
  8.5 0.9 pad_maximum_fusion.1
  9.4 0.1 reshape.88
  9.5 0.9 pad_maximum_fusion
  10.5 0.1 reshape.87
  10.6 26.4 %all-gather = bf16[16,3,4096]{2,1,0:T(4,128)(2,1)} all-gather(bf16[1,3,4096]{2,1,0:T(4,128)(2,1)} %bitcast.55), channel_id=1, replica_groups=mesh['groups'=2,'ctx'=16] {'ctx'}, dimensions={0}, use_global_device_ids=true | all-gather | bytes 417792 | tf_op jit(solution)/shard_map/all_gather | solution.py:35
  37.0 2.2 reshape.89
  39.2 0.7 fusion.36
  39.9 2.6 fusion.46
  42.5 57.8 %pmax.7 = f32[48,32]{0,1:T(8,128)S(1)} all-reduce(f32[48,32]{0,1:T(8,128)S(1)} %bitcast.53), channel_id=1, replica_groups=mesh['groups'=2,'ctx'=16] {'ctx'}, use_global_device_ids=true, to_apply=%region_1.2 | all-reduce | flops 1536 | bytes 12288 | tf_op jit(solution)/shard_map/pmax | solution.py:68
  100.3 0.0 copy-start.1
  100.3 2.1 fusion.10
  102.3 0.0 copy-done.1
  102.3 0.4 convolution_bitcast_fusion
  102.8 1.1 copy.35
  103.9 57.6 %psum.7 = f32[48,32]{0,1:T(8,128)S(1)} all-reduce(f32[48,32]{0,1:T(8,128)S(1)} %bitcast_multiply_fusion.1), channel_id=1, replica_groups=mesh['groups'=2,'ctx'=16] {'ctx'}, use_global_device_ids=true, to_apply=%region_3.4 | all-reduce | flops 1536 | bytes 12288 | tf_op jit(solution)/shard_map/psum | solution.py:70
  161.6 0.1 copy.36
  161.7 0.3 mul.72
  161.9 0.0 copy-start.3
  161.9 3.1 bitcast_multiply_fusion
  165.0 0.0 copy-start.4
  165.0 0.0 copy-start.6
  165.0 0.0 copy-start.5
  165.0 0.0 copy-start.2
  165.0 0.0 reduce-scatter.2.cloned.1.call-update
  165.1 0.0 all-reduce.3.cloned.1.call-start
  165.1 0.0 copy-done.3
  165.1 0.1 eq.30
  165.2 0.2 convert_reduce_fusion.1
  165.4 0.1 reduce_sum.49
  165.5 53.7 %reduce-scatter.2.cloned.1.call-done = f32[48,256]{1,0:T(8,128)} async-done(((f32[48,4096]{1,0:T(8,128)}), f32[48,256]{1,0:T(8,128)}) %reduce-scatter.2.cloned.1.call-update) | async-done | bytes 49168 | tf_op jit(solution)/shard_map/reduce_scatter | solution.py:72
  219.2 2.3 fusion.37
  221.5 0.0 all-reduce.3.cloned.1.call-update
  221.5 0.0 copy-done.4
  221.6 0.0 copy-done.6
  221.6 0.6 dynamic-slice
  222.8 0.0 copy-done.5
  222.8 0.7 convert_reduce_fusion
  223.5 89.5 %all-reduce.3.cloned.1.call-done = f32[48,2048]{1,0:T(8,128)} async-done(((f32[48,2048]{1,0:T(8,128)}), f32[48,2048]{1,0:T(8,128)}) %all-reduce.3.cloned.1.call-update) | async-done | bytes 393232
  313.0 0.0 copy-done.2
  313.0 1.0 multiply_reduce_fusion
  314.0 1.2 convolution_convert_fusion
  315.2 0.8 reshape.93
  316.0 13.8 %all_to_all.10 = bf16[16,3,2048]{2,1,0:T(4,128)(2,1)S(1)} all-to-all(bf16[16,3,2048]{2,1,0:T(4,128)(2,1)} %reshape.93), channel_id=1, replica_groups=mesh['groups'=2,'ctx'=16] {'ctx'}, dimensions={0} | all-to-all | bytes 393216 | tf_op jit(solution)/shard_map/all_to_all | solution.py:101
  329.8 2.6 fusion.4
  332.4 0.0 copy-done
  332.4 3.9 %fusion.6 = bf16[16,3,2048]{2,0,1:T(8,128)(2,1)} fusion(bf16[1,768,2048]{2,1,0:T(8,128)(2,1)S(1)} %copy-done, bf16[1,2048,768]{2,1,0:T(8,128)(2,1)} %param.24, f32[16,3,768]{2,0,1:T(8,128)S(1)} %fusion.4, bf16[16,3,2048]{2,1,0:T(4,128)(2,1)S(1)} %all_to_all.10), kind=kOutput, calls=%fused_computation.6 | convolution fusion | flops 302309376 | bytes 6832128 | tf_op jit(solution)/shard_map/scf,fd->scd/dot_general | solution.py:107
  336.3 1.1 copy.39
  337.4 12.7 %all_to_all.11 = bf16[16,3,2048]{2,1,0:T(4,128)(2,1)S(1)} all-to-all(bf16[16,3,2048]{2,1,0:T(4,128)(2,1)S(1)} %copy.39), channel_id=1, replica_groups=mesh['groups'=2,'ctx'=16] {'ctx'}, dimensions={0} | all-to-all | bytes 393216 | tf_op jit(solution)/shard_map/all_to_all | solution.py:110
  350.1 0.8 reshape.94
  351.0 1.8 fusion.9
  (5 shorter events, 0.0 us)
Async XLA Ops:
  6.5 325.9 %copy-start = (bf16[1,768,2048]{2,1,0:T(8,128)(2,1)S(1)}, bf16[1,768,2048]{2,1,0:T(8,128)(2,1)}, u32[]{:S(2)}) copy-start(bf16[1,768,2048]{2,1,0:T(8,128)(2,1)} %param.25) | copy-start | bytes 9437188
  6.5 212.7 %reduce-scatter.2.cloned.1.call-start = ((), (), s32[]{:S(2)}) async-start(), calls=%async_computation.3 | async-start | bytes 835584 | tf_op jit(solution)/shard_map/reduce_scatter | solution.py:72
  100.3 2.1 copy-start.1
  161.9 3.2 copy-start.3
  165.0 56.5 %copy-start.4 = (bf16[2048]{0:T(1024)(128)(2,1)S(1)}, bf16[2048]{0:T(1024)(128)(2,1)}, u32[]{:S(2)}) copy-start(bf16[2048]{0:T(1024)(128)(2,1)} %param.22) | copy-start | bytes 12292
  165.0 56.5 %copy-start.6 = (u32[32]{0:T(128)S(1)}, u32[32]{0:T(128)}, u32[]{:S(2)}) copy-start(u32[32]{0:T(128)} %constant.43) | copy-start | bytes 388
  165.0 57.8 %copy-start.5 = (f32[3,8]{1,0:T(4,128)S(1)}, f32[3,8]{1,0:T(4,128)}, u32[]{:S(2)}) copy-start(f32[3,8]{1,0:T(4,128)} %param.27) | copy-start | bytes 292
  165.0 147.9 %copy-start.2 = (bf16[3,2048]{1,0:T(4,128)(2,1)S(1)}, bf16[3,2048]{1,0:T(4,128)(2,1)}, u32[]{:S(2)}) copy-start(bf16[3,2048]{1,0:T(4,128)(2,1)} %param.20) | copy-start | bytes 36868
  165.1 147.9 %all-reduce.3.cloned.1.call-start = ((), (), s32[]{:S(2)}) async-start(), calls=%async_computation.4 | async-start | bytes 786432
Sparse Core Ops, SparseCore 0:
  165.2 53.9 reduce-scatter.1
  222.5 90.3 all-reduce.2
where the time goes:
time: 360 us
  blocking collectives  168 us (47%)
  waiting for transfers between devices  143 us (40%)
  between operations  15 us (4%)
  matrix products  14.8 us (4%)
  other arithmetic  10.8 us (3%)
  local copies, waits for them, and re-layouts  7.41 us (2%)
    unnamed x3, waiting for transfers between devices  89.5 us
    pmax x1, blocking collectives, local(): largest = lax.pmax(maxima, 'ctx')  57.8 us
    psum x1, blocking collectives, local(): denoms = lax.psum(totals * rescale, 'ctx')  57.6 us
    reduce_scatter x1, waiting for transfers between devices, local(): lax.psum_scatter(weighted, 'ctx', scatter_dimension=1, tiled=True)  53.7 us
    all_gather x1, blocking collectives, local(): whole_queries = lax.all_gather(queries, 'ctx', axis=0, tiled=True)  26.4 us
    all_to_all x1, blocking collectives, local(): lax.all_to_all(outgoing, 'ctx', split_axis=0, concat_axis=0, tiled=True)  13.8 us
    all_to_all x1, blocking collectives, local(): lax.all_to_all(expert_out, 'ctx', split_axis=0, concat_axis=0, tiled=True)  12.7 us
  transfers between devices with their start and end apart: 2, of which 2 were waited for; matrix products, arithmetic and copies ran while one was open for 0% of the time, Pallas kernels for 0%

commit v1 on v0

--- a/solution.py
+++ b/solution.py
@@ -9,6 +9,12 @@
 TOP = 8
 MASKED = -1e30
 epsilon = 1e-06
+
+
+def _end_views(inputs):
+    extra = jax.lax.all_gather(inputs, "ctx")
+    y_new = jnp.sum(extra, 0)
+    return y_new
 
 
 def local(
@@ -67,7 +73,7 @@
     totals = totals.transpose(2, 0, 1).reshape(all_rows, HEADS)
     largest = lax.pmax(maxima, "ctx")
     rescale = jnp.exp(maxima - largest)
-    denoms = lax.psum(totals * rescale, "ctx")
+    denoms = _end_views(totals * rescale)
     weighted = (numerators * (rescale / denoms)[..., None]).reshape(all_rows, HEADS * HEAD_DIM)
     columns = lax.psum_scatter(weighted, "ctx", scatter_dimension=1, tiled=True).astype(
         jnp.bfloat16

time: 360 us -> 321 us (0.89)
  blocking collectives: 168 us -> 129 us
    psum x1 -> x0, blocking collectives: 57.6 us -> none  [local(): denoms = lax.psum(totals * rescale, 'ctx')]
    all_gather x0 -> x1, blocking collectives: none -> 17.8 us  [_end_views(): extra = jax.lax.all_gather(inputs, 'ctx')]
  transfers between devices with their start and end apart: 2 -> 2, of which waited for: 2 -> 2; matrix products, arithmetic and copies ran while one was open for 0% -> 1% of each run, Pallas kernels for 0% -> 0%
where the time goes in v1:
time: 321 us; the launch traced here: 320 us
  waiting for transfers between devices  145 us (45%)
  blocking collectives  129 us (40%)
  between operations  15 us (5%)
  matrix products  14.9 us (5%)
  other arithmetic  9.13 us (3%)
  local copies, waits for them, and re-layouts  8.06 us (3%)
    unnamed x3, waiting for transfers between devices  89.5 us
    pmax x1, blocking collectives, local(): largest = lax.pmax(maxima, 'ctx')  57.8 us
    reduce_scatter x1, waiting for transfers between devices, local(): lax.psum_scatter(weighted, 'ctx', scatter_dimension=1, tiled=True)  55.3 us
    all_gather x1, blocking collectives, local(): whole_queries = lax.all_gather(queries, 'ctx', axis=0, tiled=True)  26.4 us
    all_gather x1, blocking collectives, _end_views(): extra = jax.lax.all_gather(inputs, 'ctx')  17.8 us
    all_to_all x1, blocking collectives, local(): lax.all_to_all(outgoing, 'ctx', split_axis=0, concat_axis=0, tiled=True)  13.8 us
    all_to_all x1, blocking collectives, local(): lax.all_to_all(expert_out, 'ctx', split_axis=0, concat_axis=0, tiled=True)  12.7 us
  transfers between devices with their start and end apart: 2, of which 2 were waited for; matrix products, arithmetic and copies ran while one was open for 1% of the time, Pallas kernels for 0%

profile of v1, /device:TPU:0, one launch (start us, length us, event | category | flops | bytes accessed | tf_op | source)
XLA Modules:
  0.0 320.5 jit_solution(16930446571297200287)
XLA Ops:
  6.5 0.0 copy-start
  6.5 0.0 reduce-scatter.2.cloned.1.call-start
  7.4 1.1 pad_maximum_fusion.1
  8.4 0.7 reshape.88
  9.2 0.9 pad_maximum_fusion
  10.1 0.1 reshape.87
  10.2 26.4 %all-gather.1 = bf16[16,3,4096]{2,1,0:T(4,128)(2,1)} all-gather(bf16[1,3,4096]{2,1,0:T(4,128)(2,1)} %bitcast.59), channel_id=1, replica_groups=mesh['groups'=2,'ctx'=16] {'ctx'}, dimensions={0}, use_global_device_ids=true | all-gather | bytes 417792 | tf_op jit(solution)/shard_map/all_gather | solution.py:41
  36.6 2.2 reshape.89
  38.8 2.7 fusion.47
  41.5 57.8 %pmax.7 = f32[48,32]{0,1:T(8,128)S(1)} all-reduce(f32[48,32]{0,1:T(8,128)S(1)} %bitcast.57), channel_id=1, replica_groups=mesh['groups'=2,'ctx'=16] {'ctx'}, use_global_device_ids=true, to_apply=%region_1.2 | all-reduce | flops 1536 | bytes 12288 | tf_op jit(solution)/shard_map/pmax | solution.py:74
  99.3 0.0 copy-start.1
  99.3 2.0 fusion.10
  101.4 0.0 copy-done.1
  101.4 0.4 convolution_bitcast_fusion
  101.8 1.1 copy.35
  103.0 17.8 %all-gather.2 = f32[16,48,32]{1,2,0:T(8,128)S(1)} all-gather(f32[1,48,32]{1,2,0:T(8,128)S(1)} %fusion.39), channel_id=2, replica_groups=mesh['groups'=2,'ctx'=16] {'ctx'}, dimensions={0}, use_global_device_ids=true | all-gather | bytes 104448 | tf_op jit(solution)/shard_map/all_gather | solution.py:15
  120.9 0.1 copy.36
  121.0 0.3 mul.72
  121.2 0.0 copy-start.3
  121.2 3.1 bitcast_multiply_fusion
  124.3 0.0 copy-start.4
  124.3 0.0 copy-start.6
  124.3 0.0 copy-start.5
  124.3 0.0 copy-start.2
  124.3 0.0 reduce-scatter.2.cloned.1.call-update
  124.4 0.0 all-reduce.3.cloned.1.call-start
  124.4 0.0 copy-done.3
  124.4 0.1 eq.30
  124.5 0.2 convert_reduce_fusion.1
  124.7 0.1 reduce_sum.59
  124.8 55.3 %reduce-scatter.2.cloned.1.call-done = f32[48,256]{1,0:T(8,128)} async-done(((f32[48,4096]{1,0:T(8,128)}), f32[48,256]{1,0:T(8,128)}) %reduce-scatter.2.cloned.1.call-update) | async-done | bytes 49168 | tf_op jit(solution)/shard_map/reduce_scatter | solution.py:78
  180.1 2.3 fusion.37
  182.4 0.0 all-reduce.3.cloned.1.call-update
  182.4 0.0 copy-done.4
  182.5 0.0 copy-done.6
  182.5 0.6 dynamic-slice
  183.7 0.0 copy-done.5
  183.7 0.7 convert_reduce_fusion
  184.4 89.5 %all-reduce.3.cloned.1.call-done = f32[48,2048]{1,0:T(8,128)} async-done(((f32[48,2048]{1,0:T(8,128)}), f32[48,2048]{1,0:T(8,128)}) %all-reduce.3.cloned.1.call-update) | async-done | bytes 393232
  273.9 0.0 copy-done.2
  273.9 1.0 multiply_reduce_fusion
  274.9 1.2 convolution_convert_fusion
  276.1 0.8 reshape.93
  276.9 13.8 %all_to_all.10 = bf16[16,3,2048]{2,1,0:T(4,128)(2,1)S(1)} all-to-all(bf16[16,3,2048]{2,1,0:T(4,128)(2,1)} %reshape.93), channel_id=1, replica_groups=mesh['groups'=2,'ctx'=16] {'ctx'}, dimensions={0} | all-to-all | bytes 393216 | tf_op jit(solution)/shard_map/all_to_all | solution.py:107
  290.7 2.6 fusion.4
  293.3 0.0 copy-done
  293.3 3.9 %fusion.6 = bf16[16,3,2048]{2,0,1:T(8,128)(2,1)} fusion(bf16[1,768,2048]{2,1,0:T(8,128)(2,1)S(1)} %copy-done, bf16[1,2048,768]{2,1,0:T(8,128)(2,1)} %param.24, f32[16,3,768]{2,0,1:T(8,128)S(1)} %fusion.4, bf16[16,3,2048]{2,1,0:T(4,128)(2,1)S(1)} %all_to_all.10), kind=kOutput, calls=%fused_computation.6 | convolution fusion | flops 302309376 | bytes 6832128 | tf_op jit(solution)/shard_map/scf,fd->scd/dot_general | solution.py:113
  297.2 1.1 copy.39
  298.3 12.7 %all_to_all.11 = bf16[16,3,2048]{2,1,0:T(4,128)(2,1)S(1)} all-to-all(bf16[16,3,2048]{2,1,0:T(4,128)(2,1)S(1)} %copy.39), channel_id=1, replica_groups=mesh['groups'=2,'ctx'=16] {'ctx'}, dimensions={0} | all-to-all | bytes 393216 | tf_op jit(solution)/shard_map/all_to_all | solution.py:116
  311.0 0.8 reshape.94
  311.8 1.8 fusion.9
  (9 shorter events, 0.1 us)
Async XLA Ops:
  6.5 286.7 %copy-start = (bf16[1,768,2048]{2,1,0:T(8,128)(2,1)S(1)}, bf16[1,768,2048]{2,1,0:T(8,128)(2,1)}, u32[]{:S(2)}) copy-start(bf16[1,768,2048]{2,1,0:T(8,128)(2,1)} %param.25) | copy-start | bytes 9437188
  6.5 173.6 %reduce-scatter.2.cloned.1.call-start = ((), (), s32[]{:S(2)}) async-start(), calls=%async_computation.3 | async-start | bytes 835584 | tf_op jit(solution)/shard_map/reduce_scatter | solution.py:78
  99.3 2.1 copy-start.1
  121.2 3.2 copy-start.3
  124.3 58.1 %copy-start.4 = (bf16[2048]{0:T(1024)(128)(2,1)S(1)}, bf16[2048]{0:T(1024)(128)(2,1)}, u32[]{:S(2)}) copy-start(bf16[2048]{0:T(1024)(128)(2,1)} %param.22) | copy-start | bytes 12292
  124.3 58.1 %copy-start.6 = (u32[32]{0:T(128)S(1)}, u32[32]{0:T(128)}, u32[]{:S(2)}) copy-start(u32[32]{0:T(128)} %constant.43) | copy-start | bytes 388
  124.3 59.4 %copy-start.5 = (f32[3,8]{1,0:T(4,128)S(1)}, f32[3,8]{1,0:T(4,128)}, u32[]{:S(2)}) copy-start(f32[3,8]{1,0:T(4,128)} %param.27) | copy-start | bytes 292
  124.3 149.5 %copy-start.2 = (bf16[3,2048]{1,0:T(4,128)(2,1)S(1)}, bf16[3,2048]{1,0:T(4,128)(2,1)}, u32[]{:S(2)}) copy-start(bf16[3,2048]{1,0:T(4,128)(2,1)} %param.20) | copy-start | bytes 36868
  124.4 149.5 %all-reduce.3.cloned.1.call-start = ((), (), s32[]{:S(2)}) async-start(), calls=%async_computation.4 | async-start | bytes 786432
Sparse Core Ops, SparseCore 0:
  124.5 55.5 reduce-scatter.1
  183.4 90.3 all-reduce.2
